TPU v7x, 256 devices: a whole 4x4x8 slice. The times are simulated.
256 devices in a mesh: ctx: 64 (over z, x_hi, y), tp: 4 (over x_lo, core).
Axes of the slice: x: 4 (x_hi: 2, x_lo: 2; x = x_hi * 2 + x_lo), y: 4, z: 8, core: 2. Of those that a mesh axis runs over, the one named last changes fastest.
Arguments:
- queries: bfloat16 [32768, 4096], P('ctx', 'tp'), may hold values from -22 to 22
- keys: bfloat16 [32768, 512], P('ctx', 'tp'), may hold values from -22 to 22
- values: bfloat16 [32768, 512], P('ctx', 'tp'), may hold values from -36 to 36
- positions: int32 [3, 32768], P(None, 'ctx'), may hold values from 0 to 32767
- segment_ids: int32 [32768], replicated, may hold values from 0 to 31, never falling along the last dimension, each value on 1 to 2048 neighbouring positions
- out_weight: bfloat16 [4096, 8192], P('tp', 'ctx'), may hold values from -0.09375 to 0.09375
- residual: bfloat16 [32768, 8192], P(('ctx', 'tp')), may hold values from -3 to 3
Outputs:
- layer_out: bfloat16 [32768, 8192], P(('ctx', 'tp'))
Inputs may be any that keep to these rules, and one draw needn't show every extreme that they name: `segment_ids`: ids never fall along the sequence; each document has 1 to 2048 tokens, and one has exactly 2048.
All inputs are finite; a program needn't handle non-finite values.
Results may differ from a plain program's by a relative error of at most 0.013.
Values may be sent and summed in bfloat16 or wider, within the bound.
A program may use at most 128 MiB of HBM per device.

v0:
```python
import math
import jax
import jax.numpy as jnp
from jax import lax
from jax.sharding import PartitionSpec as P

HD = 128
DOC = 2048
theta_base = 1000000.0


def from_behind(block, axis, distance):
    devices = range(lax.axis_size(axis))
    route = [(i - distance, i) for i in devices if i - distance in devices]
    return lax.ppermute(block, axis, route)


def rotary_tables(positions):
    half_dim = HD // 2
    freq_index = jnp.arange(half_dim)
    inv_freq = theta_base ** (-2.0 * freq_index.astype(jnp.float32) / HD)
    first_end = HD // 8
    second_end = first_end + 3 * HD // 16
    place = positions.astype(jnp.float32)
    chosen = jnp.where(
        freq_index[None, :] < first_end,
        place[0][:, None],
        jnp.where(freq_index[None, :] < second_end, place[1][:, None], place[2][:, None]),
    )
    angle = chosen * inv_freq[None, :]
    return (jnp.cos(angle), jnp.sin(angle))


def rotate(vectors, cosine_table, sine_table):
    half_dim = HD // 2
    lower_half = vectors[..., :half_dim]
    upper_half = vectors[..., half_dim:]
    cos_b = cosine_table[:, None, :]
    sin_b = sine_table[:, None, :]
    return jnp.concatenate(
        [lower_half * cos_b - upper_half * sin_b, upper_half * cos_b + lower_half * sin_b], axis=-1
    )


def on_device(queries, keys, values, positions, segment_ids, out_weight, residual):
    tok_rows = queries.shape[0]
    local_heads = queries.shape[1] // HD
    local_kv = keys.shape[1] // HD
    group_size = local_heads // local_kv
    reach_blocks = (DOC + tok_rows - 2) // tok_rows
    my_start = lax.axis_index("ctx") * tok_rows
    cosine_table, sine_table = rotary_tables(positions)
    rot_q = rotate(
        queries.reshape(tok_rows, local_heads, HD).astype(jnp.float32), cosine_table, sine_table
    ).astype(jnp.bfloat16)
    grouped = rot_q.reshape(tok_rows, local_kv, group_size, HD).transpose(1, 2, 0, 3)
    rot_k = rotate(
        keys.reshape(tok_rows, local_kv, HD).astype(jnp.float32), cosine_table, sine_table
    ).astype(jnp.bfloat16)
    key_flat = rot_k.reshape(tok_rows, local_kv * HD)
    query_index = my_start + jnp.arange(tok_rows, dtype=jnp.int32)
    query_seg = lax.dynamic_slice_in_dim(segment_ids, my_start, tok_rows, 0)
    score_scale = 1.0 / math.sqrt(HD)
    block_rows = math.gcd(tok_rows, 512)
    block_count = tok_rows // block_rows

    def absorb(running, stacked, offset):
        key_blocks = stacked[0].reshape(block_count, block_rows, local_kv, HD)
        value_blocks = stacked[1].reshape(block_count, block_rows, local_kv, HD)

        def advance(block_index, carried):
            key_block = lax.dynamic_index_in_dim(key_blocks, block_index, 0, keepdims=False)
            value_block = lax.dynamic_index_in_dim(value_blocks, block_index, 0, keepdims=False)
            key_first = offset + block_index * block_rows
            key_index = key_first + jnp.arange(block_rows, dtype=jnp.int32)
            key_seg = lax.dynamic_slice_in_dim(
                segment_ids, jnp.maximum(key_first, 0), block_rows, 0
            )
            allowed = (
                (key_index[None, :] <= query_index[:, None])
                & (key_index[None, :] >= 0)
                & (key_seg[None, :] == query_seg[:, None])
            )

            def update(current):
                row_peak, row_sum, weighted = current
                score = (
                    jnp.einsum(
                        "kgtd,nkd->kgtn", grouped, key_block, preferred_element_type=jnp.float32
                    )
                    * score_scale
                )
                score = jnp.where(allowed, score, -1e30)
                new_peak = jnp.maximum(row_peak, jnp.max(score, axis=-1))
                prob = jnp.where(allowed, jnp.exp(score - new_peak[..., None]), 0.0)
                rescale = jnp.exp(row_peak - new_peak)
                row_sum = row_sum * rescale + jnp.sum(prob, axis=-1)
                weighted = weighted * rescale[..., None] + jnp.einsum(
                    "kgtn,nkd->kgtd",
                    prob.astype(jnp.bfloat16),
                    value_block,
                    preferred_element_type=jnp.float32,
                )
                return (new_peak, row_sum, weighted)

            def keep_state(current):
                return current

            return lax.cond(jnp.any(allowed), update, keep_state, carried)

        return lax.fori_loop(0, block_count, advance, running)

    initial = (
        jnp.full((local_kv, group_size, tok_rows), -1e30, jnp.float32),
        jnp.zeros((local_kv, group_size, tok_rows), jnp.float32),
        jnp.zeros((local_kv, group_size, tok_rows, HD), jnp.float32),
    )
    own_pair = jnp.stack([key_flat, values], axis=0)
    state = absorb(initial, own_pair, my_start)

    def next_block(step_index, carried):
        moving, running = carried
        moving = from_behind(moving, "ctx", 1)
        running = absorb(running, moving, my_start - step_index * tok_rows)
        return (moving, running)

    moving, state = lax.fori_loop(1, reach_blocks + 1, next_block, (own_pair, state))
    row_peak, row_sum, weighted = state
    attended = (
        (weighted / row_sum[..., None])
        .transpose(2, 0, 1, 3)
        .reshape(tok_rows, local_heads * HD)
        .astype(jnp.bfloat16)
    )
    partial_sum = jnp.dot(
        attended,
        lax.all_gather(out_weight, "ctx", axis=1, tiled=True),
        preferred_element_type=jnp.float32,
    )
    partial_sum = partial_sum.astype(jnp.bfloat16).astype(jnp.float32)
    shared = lax.psum_scatter(
        partial_sum.astype(jnp.bfloat16), "tp", scatter_dimension=0, tiled=True
    ).astype(jnp.float32)
    return (shared + residual.astype(jnp.float32)).astype(jnp.bfloat16)


def solution(mesh):
    return jax.shard_map(
        on_device,
        mesh=mesh,
        in_specs=(
            P("ctx", "tp"),
            P("ctx", "tp"),
            P("ctx", "tp"),
            P(None, "ctx"),
            P(),
            P("tp", "ctx"),
            P(("ctx", "tp"), None),
        ),
        out_specs=P(("ctx", "tp"), None),
        check_vma=False,
    )
```

profile of v0, /device:TPU:1, one launch (start us, length us, event | category | flops | bytes accessed | tf_op | source)
XLA Modules:
  0.0 394.7 jit_solution(13520080402836505690)
XLA Ops:
  6.5 0.0 all-gather.2.cloned.1.call-start
  6.5 0.7 all-gather.2.cloned.1.call-update
  7.3 0.0 reduce-scatter.2.cloned.1.call-start
  7.3 0.7 convert_element_type.93
  8.0 1.5 copy.12
  9.5 0.3 convert.25
  9.8 0.8 fusion.44
  10.7 1.0 fusion.43
  12.4 0.6 fusion.41
  13.0 0.3 fusion.36
  13.4 0.1 maximum_bitcast_fusion
  13.5 0.7 copy.14
  14.2 1.5 broadcast_in_dim.135
  15.7 2.2 subtract_convert_fusion.1
  17.9 0.1 pad_maximum_fusion.1
  18.0 8.1 %conditional.2 = ((f32[1,8,512]{2,1,0:T(8,128)S(1)}, f32[1,8,512]{2,1,0:T(8,128)S(1)}, f32[1,8,512,128]{3,2,1,0:T(8,128)})) conditional(s32[]{:T(128)} %convert_element_type.95, (f32[1,8,512]{2,1,0:T(8,128)S(1)}, f32[1,8,512]{2,1,0:T(8,128)S(1)}, f32[1,8,512,128]{3,2,1,0:T(8,128)}) %tuple.39, (pred[512,512]{0,1:T(8,128)(4,1)S(1)}, ...), branch_computations={%region_1.2_spmd, %region_2.0_spmd} | conditional | flops 1102065664 | bytes 49021044 | solution.py:109
  18.0 0.0 copy-start
  18.0 0.0 copy-start.6
  18.0 1.5 fusion.2
  19.6 2.0 fusion.4
  21.6 3.1 bitcast_add_fusion
  24.8 0.0 copy-start.1
  24.8 1.3 copy-done.1
  26.1 1.0 pad_maximum_fusion
  27.1 47.2 %while.28 = (s32[]{:T(128)}, bf16[2,512,128]{2,1,0:T(8,128)(2,1)S(1)}, f32[1,8,512]{2,1,0:T(8,128)S(1)}, f32[1,8,512]{2,1,0:T(8,128)S(1)}, f32[1,8,512,128]{3,2,...) while((s32[]{:T(128)}, ...), condition=%wide.region_11.12_spmd.clone.clone, body=%wide.region_5.11_spmd.clone.clone.sunk | while | flops 1103378432 | bytes 50349432 | solution.py:127
  27.2 4.0 %collective-permute-start = (bf16[2,512,128]{2,1,0:T(8,128)(2,1)S(1)}, bf16[2,512,128]{2,1,0:T(8,128)(2,1)S(1)}, u32[]{:S(2)}, u32[]{:S(2)}) collective-permute-start(bf16[2,512,128]{2,1,0:T(8,128)(2,1)S(1)} %get-tuple-element.546), channel_id=1, source_target_pairs={{0,4},{4,8},{8,12},{12,16},{16,20},{20,24},{24,28},{28,32},{32,36}... | collective-permute-start | bytes 786440 | tf_op jit(solution)/shard_map/while/body/eval_jaxpr/ppermute | solution.py:15
  31.3 0.8 dynamic_slice.35
  32.0 1.1 fusion.49
  33.8 2.9 collective-permute-done
  36.7 11.1 %collective-permute-start = (bf16[2,512,128]{2,1,0:T(8,128)(2,1)S(1)}, bf16[2,512,128]{2,1,0:T(8,128)(2,1)S(1)}, u32[]{:S(2)}, u32[]{:S(2)}) collective-permute-start(bf16[2,512,128]{2,1,0:T(8,128)(2,1)S(1)} %get-tuple-element.546), channel_id=1, source_target_pairs={{0,4},{4,8},{8,12},{12,16},{16,20},{20,24},{24,28},{28,32},{32,36}... | collective-permute-start | bytes 786440 | tf_op jit(solution)/shard_map/while/body/eval_jaxpr/ppermute | solution.py:15
  47.8 0.8 dynamic_slice.35
  48.6 1.1 fusion.49
  50.4 0.7 collective-permute-done
  51.1 3.8 collective-permute-start
  55.0 0.8 dynamic_slice.35
  55.8 1.1 fusion.49
  57.5 0.7 collective-permute-done
  58.3 12.8 %collective-permute-start = (bf16[2,512,128]{2,1,0:T(8,128)(2,1)S(1)}, bf16[2,512,128]{2,1,0:T(8,128)(2,1)S(1)}, u32[]{:S(2)}, u32[]{:S(2)}) collective-permute-start(bf16[2,512,128]{2,1,0:T(8,128)(2,1)S(1)} %get-tuple-element.546), channel_id=1, source_target_pairs={{0,4},{4,8},{8,12},{12,16},{16,20},{20,24},{24,28},{28,32},{32,36}... | collective-permute-start | bytes 786440 | tf_op jit(solution)/shard_map/while/body/eval_jaxpr/ppermute | solution.py:15
  71.1 0.8 dynamic_slice.35
  71.9 1.1 fusion.49
  73.7 0.7 collective-permute-done
  74.4 1.9 copy.15
  76.3 0.3 divide_convert_fusion
  76.6 209.5 %all-gather.2.cloned.1.call-done = bf16[1024,8192]{1,0:T(8,128)(2,1)} async-done(((bf16[1024,128]{1,0:T(8,128)(2,1)}), bf16[1024,8192]{1,0:T(8,128)(2,1)}) %all-gather.2.cloned.1.call-update) | async-done | bytes 16777232 | tf_op jit(solution)/shard_map/all_gather | solution.py:137
  286.1 16.9 %convolution_convert_fusion = bf16[512,8192]{1,0:T(8,128)(2,1)} fusion(bf16[512,1024]{0,1:T(8,128)(2,1)S(1)} %bitcast.79, bf16[1024,8192]{1,0:T(8,128)(2,1)} %all-gather.2.cloned.1.call-done), kind=kOutput, calls=%fused_computation.45 | convolution fusion | flops 8594128896 | bytes 26214400 | tf_op jit(solution)/shard_map/dot_general | solution.py:135
  303.1 0.0 reduce-scatter.2.cloned.1.call-update
  303.1 81.3 %reduce-scatter.2.cloned.1.call-done = bf16[128,8192]{1,0:T(8,128)(2,1)} async-done(((bf16[512,8192]{1,0:T(8,128)(2,1)}), bf16[128,8192]{1,0:T(8,128)(2,1)}) %reduce-scatter.2.cloned.1.call-update) | async-done | bytes 2097168 | tf_op jit(solution)/shard_map/reduce_scatter | solution.py:141
  384.4 3.4 add_convert_fusion
  (52 shorter events, 0.3 us)
Async XLA Ops:
  6.5 9.1 %copy-start.5 = (bf16[512,128]{1,0:T(8,128)(2,1)S(1)}, bf16[512,128]{1,0:T(8,128)(2,1)}, u32[]{:S(2)}) copy-start(bf16[512,128]{1,0:T(8,128)(2,1)} %param.14) | copy-start | bytes 393220
  6.5 279.6 %all-gather.2.cloned.1.call-start = ((), (), s32[]{:S(2)}) async-start(), calls=%async_computation.1 | async-start | bytes 17039360 | tf_op jit(solution)/shard_map/all_gather | solution.py:137
  7.3 377.1 %reduce-scatter.2.cloned.1.call-start = ((), (), s32[]{:S(2)}) async-start(), calls=%async_computation.2 | async-start | bytes 10485760 | tf_op jit(solution)/shard_map/reduce_scatter | solution.py:141
  10.7 2.3 copy-start.7
  12.3 0.7 copy-start.12
  12.4 0.7 copy-start.13
  12.4 0.7 copy-start.14
  12.4 0.6 copy-start.11
  12.4 1.7 copy-start.9
  12.4 1.7 copy-start.10
  18.0 9.2 %copy-start.8 = (s32[512]{0:T(512)S(1)}, s32[512]{0:T(512)}, u32[]{:S(2)}) copy-start(s32[512]{0:T(512)} %copy-done.7) | copy-start | bytes 6148
  18.0 3.6 copy-start
  18.0 3.6 copy-start.6
  24.8 1.3 copy-start.1
  27.2 9.5 %collective-permute-start = (bf16[2,512,128]{2,1,0:T(8,128)(2,1)S(1)}, bf16[2,512,128]{2,1,0:T(8,128)(2,1)S(1)}, u32[]{:S(2)}, u32[]{:S(2)}) collective-permute-start(bf16[2,512,128]{2,1,0:T(8,128)(2,1)S(1)} %get-tuple-element.546), channel_id=1, source_target_pairs={{0,4},{4,8},{8,12},{12,16},{16,20},{20,24},{24,28},{28,32},{32,36}... | collective-permute-start | bytes 786440 | tf_op jit(solution)/shard_map/while/body/eval_jaxpr/ppermute | solution.py:15
  36.7 14.3 %collective-permute-start = (bf16[2,512,128]{2,1,0:T(8,128)(2,1)S(1)}, bf16[2,512,128]{2,1,0:T(8,128)(2,1)S(1)}, u32[]{:S(2)}, u32[]{:S(2)}) collective-permute-start(bf16[2,512,128]{2,1,0:T(8,128)(2,1)S(1)} %get-tuple-element.546), channel_id=1, source_target_pairs={{0,4},{4,8},{8,12},{12,16},{16,20},{20,24},{24,28},{28,32},{32,36}... | collective-permute-start | bytes 786440 | tf_op jit(solution)/shard_map/while/body/eval_jaxpr/ppermute | solution.py:15
  51.1 7.1 %collective-permute-start = (bf16[2,512,128]{2,1,0:T(8,128)(2,1)S(1)}, bf16[2,512,128]{2,1,0:T(8,128)(2,1)S(1)}, u32[]{:S(2)}, u32[]{:S(2)}) collective-permute-start(bf16[2,512,128]{2,1,0:T(8,128)(2,1)S(1)} %get-tuple-element.546), channel_id=1, source_target_pairs={{0,4},{4,8},{8,12},{12,16},{16,20},{20,24},{24,28},{28,32},{32,36}... | collective-permute-start | bytes 786440 | tf_op jit(solution)/shard_map/while/body/eval_jaxpr/ppermute | solution.py:15
  58.3 16.1 %collective-permute-start = (bf16[2,512,128]{2,1,0:T(8,128)(2,1)S(1)}, bf16[2,512,128]{2,1,0:T(8,128)(2,1)S(1)}, u32[]{:S(2)}, u32[]{:S(2)}) collective-permute-start(bf16[2,512,128]{2,1,0:T(8,128)(2,1)S(1)} %get-tuple-element.546), channel_id=1, source_target_pairs={{0,4},{4,8},{8,12},{12,16},{16,20},{20,24},{24,28},{28,32},{32,36}... | collective-permute-start | bytes 786440 | tf_op jit(solution)/shard_map/while/body/eval_jaxpr/ppermute | solution.py:15
  303.1 81.4 %copy-start.4 = (bf16[128,8192]{1,0:T(8,128)(2,1)S(1)}, bf16[128,8192]{1,0:T(8,128)(2,1)}, u32[]{:S(2)}) copy-start(bf16[128,8192]{1,0:T(8,128)(2,1)} %param.19) | copy-start | bytes 6291460
Sparse Core Ops, SparseCore 0:
  10.7 275.3 all-gather.1
  303.2 81.1 reduce-scatter.1
where the time goes:
time: 395 us
  waiting for transfers between devices  296 us (75%)
  starting transfers between devices  31.8 us (8%)
  matrix products  21.6 us (5%)
  other arithmetic  17.3 us (4%)
  between operations  14.3 us (4%)
  local copies, waits for them, and re-layouts  10.1 us (3%)
    all_gather x1, waiting for transfers between devices, on_device(): lax.all_gather(out_weight, 'ctx', axis=1, tiled=True)  209 us
    reduce_scatter x1, waiting for transfers between devices, on_device(): lax.psum_scatter(partial_sum.astype(jnp.bfloat16), 'tp', scatter_dimensio...  81.3 us
    ppermute x4, starting transfers between devices, from_behind(): return lax.ppermute(block, axis, route)  31.7 us
    dot_general x1, matrix products, on_device(): jnp.dot(attended, lax.all_gather(out_weight, 'ctx', axis=1, tiled=True),...  16.9 us
  transfers between devices with their start and end apart: 6, of which 6 were waited for; matrix products, arithmetic and copies ran while one was open for 7% of the time, Pallas kernels for 0%

commit v1 on v0

--- a/solution.py
+++ b/solution.py
@@ -134,7 +134,7 @@
     )
     partial_sum = jnp.dot(
         attended,
-        lax.all_gather(out_weight, "ctx", axis=1, tiled=True),
+        jnp.concatenate(lax.all_gather(out_weight, "ctx"), axis=1),
         preferred_element_type=jnp.float32,
     )
     partial_sum = partial_sum.astype(jnp.bfloat16).astype(jnp.float32)

time: 395 us -> 376 us (0.952)
  waiting for transfers between devices: 296 us -> 240 us
  local copies, waits for them, and re-layouts: 10.1 us -> 31.2 us
  matrix products: 21.6 us -> 34.4 us
  starting transfers between devices: 31.8 us -> 36 us
    all_gather x1, waiting for transfers between devices: 209 us -> 148 us  [on_device(): lax.all_gather(out_weight, 'ctx')]
    reshape x0 -> x1, local copies, waits for them, and re-layouts: none -> 22.4 us  [on_device(): jnp.concatenate(lax.all_gather(out_weight, 'ctx'), axis=1)]
    dot_general x1, matrix products: 16.9 us -> 29.8 us  [on_device(): jnp.dot(attended, jnp.concatenate(lax.all_gather(out_weight, 'ctx'), axis...]
    ppermute x4, waiting for transfers between devices: 4.86 us -> 11.2 us  [from_behind(): return lax.ppermute(block, axis, route)]
    ppermute x4, starting transfers between devices: 31.7 us -> 35.9 us  [from_behind(): return lax.ppermute(block, axis, route)]
where the time goes in v1:
time: 376 us; the launch traced here: 375 us
  waiting for transfers between devices  240 us (64%)
  starting transfers between devices  36 us (10%)
  matrix products  34.4 us (9%)
  local copies, waits for them, and re-layouts  31.2 us (8%)
  other arithmetic  16.4 us (4%)
  between operations  14.2 us (4%)
    all_gather x1, waiting for transfers between devices, on_device(): lax.all_gather(out_weight, 'ctx')  148 us
    reduce_scatter x1, waiting for transfers between devices, on_device(): lax.psum_scatter(partial_sum.astype(jnp.bfloat16), 'tp', scatter_dimensio...  79.5 us
    ppermute x4, starting transfers between devices, from_behind(): return lax.ppermute(block, axis, route)  35.9 us
    dot_general x1, matrix products, on_device(): jnp.dot(attended, jnp.concatenate(lax.all_gather(out_weight, 'ctx'), axis...  29.8 us
    reshape x1, local copies, waits for them, and re-layouts, on_device(): jnp.concatenate(lax.all_gather(out_weight, 'ctx'), axis=1)  22.4 us
    ppermute x4, waiting for transfers between devices, from_behind(): return lax.ppermute(block, axis, route)  11.2 us
  transfers between devices with their start and end apart: 6, of which 6 were waited for; matrix products, arithmetic and copies ran while one was open for 7% of the time, Pallas kernels for 0%

profile of v1, /device:TPU:1, one launch (start us, length us, event | category | flops | bytes accessed | tf_op | source)
XLA Modules:
  0.0 375.2 jit_solution(8102281250525010199)
XLA Ops:
  6.5 0.7 all-gather.3.cloned.1.call-update
  7.3 0.0 reduce-scatter.2.cloned.1.call-start
  7.3 0.7 convert_element_type.93
  8.0 0.8 fusion.44
  8.9 1.0 fusion.43
  10.5 0.0 copy-start.7
  10.5 1.5 copy.18
  12.1 0.3 convert.25
  12.4 0.6 fusion.41
  13.0 0.4 fusion.36
  13.4 0.1 maximum_bitcast_fusion
  13.4 0.7 copy.20
  14.1 1.5 broadcast_in_dim.135
  15.6 1.4 subtract_convert_fusion.1
  17.0 0.1 pad_maximum_fusion.1
  17.2 7.0 %conditional.2 = ((f32[1,8,512]{2,1,0:T(8,128)S(1)}, f32[1,8,512]{2,1,0:T(8,128)S(1)}, f32[1,8,512,128]{3,2,1,0:T(8,128)})) conditional(s32[]{:T(128)} %convert_element_type.95, (f32[1,8,512]{2,1,0:T(8,128)S(1)}, f32[1,8,512]{2,1,0:T(8,128)S(1)}, f32[1,8,512,128]{3,2,1,0:T(8,128)}) %tuple.39, (pred[512,512]{0,1:T(8,128)(4,1)S(1)}, ...), branch_computations={%region_1.2_spmd, %region_2.0_spmd} | conditional | flops 1102065664 | bytes 48496728 | solution.py:109
  17.2 0.0 copy-start
  17.2 1.5 fusion.2
  18.7 0.0 copy-done
  18.8 3.1 bitcast_add_fusion
  21.9 0.0 copy-start.1
  21.9 2.0 fusion.4
  24.2 0.1 pad_maximum_fusion
  24.3 57.3 %while.28 = (s32[]{:T(128)}, bf16[2,512,128]{2,1,0:T(8,128)(2,1)S(1)}, f32[1,8,512]{2,1,0:T(8,128)S(1)}, f32[1,8,512]{2,1,0:T(8,128)S(1)}, f32[1,8,512,128]{3,2,...) while((s32[]{:T(128)}, ...), condition=%wide.region_11.12_spmd.clone.clone, body=%wide.region_5.11_spmd.clone.clone.sunk | while | flops 1103378432 | bytes 50349432 | solution.py:127
  24.3 4.0 %collective-permute-start = (bf16[2,512,128]{2,1,0:T(8,128)(2,1)S(1)}, bf16[2,512,128]{2,1,0:T(8,128)(2,1)S(1)}, u32[]{:S(2)}, u32[]{:S(2)}) collective-permute-start(bf16[2,512,128]{2,1,0:T(8,128)(2,1)S(1)} %get-tuple-element.562), channel_id=1, source_target_pairs={{0,4},{4,8},{8,12},{12,16},{16,20},{20,24},{24,28},{28,32},{32,36}... | collective-permute-start | bytes 786440 | tf_op jit(solution)/shard_map/while/body/eval_jaxpr/ppermute | solution.py:15
  28.4 0.8 dynamic_slice.35
  29.2 1.0 fusion.49
  30.9 4.7 %collective-permute-done = bf16[2,512,128]{2,1,0:T(8,128)(2,1)S(1)} collective-permute-done((bf16[2,512,128]{2,1,0:T(8,128)(2,1)S(1)}, bf16[2,512,128]{2,1,0:T(8,128)(2,1)S(1)}, u32[]{:S(2)}, u32[]{:S(2)}) %collective-permute-start) | collective-permute-done | bytes 262176 | tf_op jit(solution)/shard_map/while/body/eval_jaxpr/ppermute | solution.py:15
  35.6 12.3 %collective-permute-start = (bf16[2,512,128]{2,1,0:T(8,128)(2,1)S(1)}, bf16[2,512,128]{2,1,0:T(8,128)(2,1)S(1)}, u32[]{:S(2)}, u32[]{:S(2)}) collective-permute-start(bf16[2,512,128]{2,1,0:T(8,128)(2,1)S(1)} %get-tuple-element.562), channel_id=1, source_target_pairs={{0,4},{4,8},{8,12},{12,16},{16,20},{20,24},{24,28},{28,32},{32,36}... | collective-permute-start | bytes 786440 | tf_op jit(solution)/shard_map/while/body/eval_jaxpr/ppermute | solution.py:15
  48.0 0.8 dynamic_slice.35
  48.7 1.0 fusion.49
  50.4 2.3 collective-permute-done
  52.7 4.2 %collective-permute-start = (bf16[2,512,128]{2,1,0:T(8,128)(2,1)S(1)}, bf16[2,512,128]{2,1,0:T(8,128)(2,1)S(1)}, u32[]{:S(2)}, u32[]{:S(2)}) collective-permute-start(bf16[2,512,128]{2,1,0:T(8,128)(2,1)S(1)} %get-tuple-element.562), channel_id=1, source_target_pairs={{0,4},{4,8},{8,12},{12,16},{16,20},{20,24},{24,28},{28,32},{32,36}... | collective-permute-start | bytes 786440 | tf_op jit(solution)/shard_map/while/body/eval_jaxpr/ppermute | solution.py:15
  57.0 0.8 dynamic_slice.35
  57.8 1.0 fusion.49
  59.4 1.5 collective-permute-done
  61.0 15.4 %collective-permute-start = (bf16[2,512,128]{2,1,0:T(8,128)(2,1)S(1)}, bf16[2,512,128]{2,1,0:T(8,128)(2,1)S(1)}, u32[]{:S(2)}, u32[]{:S(2)}) collective-permute-start(bf16[2,512,128]{2,1,0:T(8,128)(2,1)S(1)} %get-tuple-element.562), channel_id=1, source_target_pairs={{0,4},{4,8},{8,12},{12,16},{16,20},{20,24},{24,28},{28,32},{32,36}... | collective-permute-start | bytes 786440 | tf_op jit(solution)/shard_map/while/body/eval_jaxpr/ppermute | solution.py:15
  76.4 0.8 dynamic_slice.35
  77.2 1.0 fusion.49
  78.9 2.7 collective-permute-done
  81.6 1.9 copy.21
  83.6 1.2 divide_convert_fusion
  84.8 148.5 %all-gather.3.cloned.1.call-done = bf16[65536,128]{1,0:T(8,128)(2,1)} async-done(((bf16[1024,128]{1,0:T(8,128)(2,1)}), bf16[65536,128]{1,0:T(8,128)(2,1)}) %all-gather.3.cloned.1.call-update) | async-done | bytes 16777232 | tf_op jit(solution)/shard_map/all_gather | solution.py:137
  233.3 22.4 %copy.22 = bf16[1024,64,128]{0,2,1:T(8,128)(2,1)} copy(bf16[1024,64,128]{2,0,1:T(8,128)(2,1)} %bitcast.77) | data formatting | bytes 33554432 | tf_op jit(solution)/shard_map/reshape | solution.py:137
  255.7 29.8 %convolution_convert_fusion = bf16[512,8192]{1,0:T(8,128)(2,1)} fusion(bf16[512,1024]{0,1:T(8,128)(2,1)S(1)} %bitcast.85, bf16[1024,8192]{0,1:T(8,128)(2,1)} %bitcast.78), kind=kOutput, calls=%fused_computation.45 | convolution fusion | flops 8594128896 | bytes 26214400 | tf_op jit(solution)/shard_map/dot_general | solution.py:135
  285.5 0.0 reduce-scatter.2.cloned.1.call-update
  285.5 79.5 %reduce-scatter.2.cloned.1.call-done = bf16[128,8192]{1,0:T(8,128)(2,1)} async-done(((bf16[512,8192]{1,0:T(8,128)(2,1)}), bf16[128,8192]{1,0:T(8,128)(2,1)}) %reduce-scatter.2.cloned.1.call-update) | async-done | bytes 2097168 | tf_op jit(solution)/shard_map/reduce_scatter | solution.py:141
  365.0 3.4 add_convert_fusion
  (39 shorter events, 0.2 us)
Async XLA Ops:
  6.5 9.1 %copy-start.6 = (bf16[512,128]{1,0:T(8,128)(2,1)S(1)}, bf16[512,128]{1,0:T(8,128)(2,1)}, u32[]{:S(2)}) copy-start(bf16[512,128]{1,0:T(8,128)(2,1)} %param.14) | copy-start | bytes 393220
  6.5 226.8 %all-gather.3.cloned.1.call-start = ((), (), s32[]{:S(2)}) async-start(), calls=%async_computation.2 | async-start | bytes 17039360 | tf_op jit(solution)/shard_map/all_gather | solution.py:137
  7.3 357.7 %reduce-scatter.2.cloned.1.call-start = ((), (), s32[]{:S(2)}) async-start(), calls=%async_computation.1 | async-start | bytes 10485760 | tf_op jit(solution)/shard_map/reduce_scatter | solution.py:141
  10.5 6.6 %copy-start.7 = (bf16[512,128]{1,0:T(8,128)(2,1)S(1)}, bf16[512,128]{1,0:T(8,128)(2,1)}, u32[]{:S(2)}) copy-start(bf16[512,128]{1,0:T(8,128)(2,1)} %param.15) | copy-start | bytes 393220
  17.2 1.6 copy-start
  21.9 2.1 copy-start.1
  24.3 11.2 %collective-permute-start = (bf16[2,512,128]{2,1,0:T(8,128)(2,1)S(1)}, bf16[2,512,128]{2,1,0:T(8,128)(2,1)S(1)}, u32[]{:S(2)}, u32[]{:S(2)}) collective-permute-start(bf16[2,512,128]{2,1,0:T(8,128)(2,1)S(1)} %get-tuple-element.562), channel_id=1, source_target_pairs={{0,4},{4,8},{8,12},{12,16},{16,20},{20,24},{24,28},{28,32},{32,36}... | collective-permute-start | bytes 786440 | tf_op jit(solution)/shard_map/while/body/eval_jaxpr/ppermute | solution.py:15
  35.6 17.1 %collective-permute-start = (bf16[2,512,128]{2,1,0:T(8,128)(2,1)S(1)}, bf16[2,512,128]{2,1,0:T(8,128)(2,1)S(1)}, u32[]{:S(2)}, u32[]{:S(2)}) collective-permute-start(bf16[2,512,128]{2,1,0:T(8,128)(2,1)S(1)} %get-tuple-element.562), channel_id=1, source_target_pairs={{0,4},{4,8},{8,12},{12,16},{16,20},{20,24},{24,28},{28,32},{32,36}... | collective-permute-start | bytes 786440 | tf_op jit(solution)/shard_map/while/body/eval_jaxpr/ppermute | solution.py:15
  52.7 8.2 %collective-permute-start = (bf16[2,512,128]{2,1,0:T(8,128)(2,1)S(1)}, bf16[2,512,128]{2,1,0:T(8,128)(2,1)S(1)}, u32[]{:S(2)}, u32[]{:S(2)}) collective-permute-start(bf16[2,512,128]{2,1,0:T(8,128)(2,1)S(1)} %get-tuple-element.562), channel_id=1, source_target_pairs={{0,4},{4,8},{8,12},{12,16},{16,20},{20,24},{24,28},{28,32},{32,36}... | collective-permute-start | bytes 786440 | tf_op jit(solution)/shard_map/while/body/eval_jaxpr/ppermute | solution.py:15
  61.0 20.6 %collective-permute-start = (bf16[2,512,128]{2,1,0:T(8,128)(2,1)S(1)}, bf16[2,512,128]{2,1,0:T(8,128)(2,1)S(1)}, u32[]{:S(2)}, u32[]{:S(2)}) collective-permute-start(bf16[2,512,128]{2,1,0:T(8,128)(2,1)S(1)} %get-tuple-element.562), channel_id=1, source_target_pairs={{0,4},{4,8},{8,12},{12,16},{16,20},{20,24},{24,28},{28,32},{32,36}... | collective-permute-start | bytes 786440 | tf_op jit(solution)/shard_map/while/body/eval_jaxpr/ppermute | solution.py:15
  233.3 22.4 %copy-start.5 = (bf16[1,8,512,128]{2,3,1,0:T(8,128)(2,1)S(1)}, bf16[1,8,512,128]{2,3,1,0:T(8,128)(2,1)}, u32[]{:S(2)}) copy-start(bf16[1,8,512,128]{2,3,1,0:T(8,128)(2,1)} %divide_convert_fusion) | copy-start | bytes 3145732
  285.5 79.5 %copy-start.4 = (bf16[128,8192]{1,0:T(8,128)(2,1)S(1)}, bf16[128,8192]{1,0:T(8,128)(2,1)}, u32[]{:S(2)}) copy-start(bf16[128,8192]{1,0:T(8,128)(2,1)} %param.19) | copy-start | bytes 6291460
Sparse Core Ops, SparseCore 0:
  10.8 222.4 all-gather.2
  285.6 79.3 reduce-scatter.1
